TPU v7x, 32 devices: a whole 2x2x4 slice. The times are simulated.
32 devices in a mesh: ka: 4 (over y, x), ga: 8 (over z, core).
Axes of the slice: x: 2, y: 2, z: 4, core: 2. Of those that a mesh axis runs over, the one named last changes fastest.
Arguments:
- orbitals: bfloat16 [8, 8, 2, 32, 1024], P('ka', None, None, 'ga'), may hold values from -6 to 6
- band_counts: int32 [8], replicated, may hold values from 1 to 8, as said below
- pair_slot: int32 [8, 8], replicated, may hold values from 0 to 7
- kernel: float32 [8, 32, 1024], P(None, None, 'ga'), may hold values from 0.2 to 8
Outputs:
- exchange_vectors: float32 [8, 8, 2, 32, 1024], P('ka', None, None, 'ga')
- exchange_matrix: float32 [8, 2, 8, 8], P('ka')
- exchange_energy: float32 [], replicated
Inputs may be any that keep to these rules, and one draw needn't show every extreme that they name: The first band_counts[k] band slots of k-point k are the occupied ones; some k-point has all 8 slots occupied.
All inputs are finite; a program needn't handle non-finite values.
Results may differ from a plain program's by a relative error of at most 0.0003.
Values may be sent and summed in bfloat16 or wider, within the bound.
A program may use at most 128 MiB of HBM per device.

v0:
```python
import jax
import jax.numpy as jnp
import numpy as np
from jax import lax
from jax.experimental import pallas as pl
from jax.experimental.pallas import tpu as pltpu
from jax.sharding import PartitionSpec as P

STEPS = 2
LANES = 128


def split_np(matrix):
    high = matrix.astype(np.float32).astype(jnp.bfloat16)
    low = (matrix - high.astype(np.float64)).astype(np.float32).astype(jnp.bfloat16)
    return high, low


def real_form(matrix):
    return np.block([[matrix.real, -matrix.imag], [matrix.imag, matrix.real]])


def build_tables(points, members):
    wide = LANES // points
    quads = points // (2 * wide)
    planes = points // members
    dft = np.exp(-2j * np.pi * np.outer(np.arange(points), np.arange(points)) / points)
    x_of = np.arange(points).reshape(members, 1, planes)
    y1_of = np.arange(quads).reshape(1, quads, 1)
    x_of, y1_of = (np.broadcast_to(v, (members, quads, planes)).reshape(-1) for v in (x_of, y1_of))
    gx = np.tile(np.arange(points), quads)
    q = np.repeat(np.arange(quads), points)
    left, left_back = [], []
    for p in range(2):
        phase = np.outer(gx, x_of) / points + np.outer(p + 2 * q, y1_of) * wide / points
        forward = np.exp(-2j * np.pi * phase)
        high, low = split_np(real_form(forward))
        left.append(np.concatenate([high, low, high], axis=1))
        high, low = split_np(real_form(np.conj(forward).T))
        left_back.append(np.concatenate([high, low, high], axis=1))
    small = np.exp(-2j * np.pi * np.outer(np.arange(wide), np.arange(wide)) / wide)
    lane = np.kron(small, dft)
    right = []
    for matrix in (lane, np.conj(lane)):
        high, low = split_np(real_form(matrix).T)
        right.append(np.concatenate([high, low, high], axis=0))
    low_freq = (np.arange(2)[:, None] + 2 * np.arange(quads)[None, :]).reshape(-1)
    y0 = np.repeat(np.arange(wide), points)
    twiddle = np.exp(-2j * np.pi * np.outer(low_freq, y0) / points)
    twiddle = np.stack([twiddle.real, twiddle.imag]).astype(np.float32)
    return np.stack(left), np.stack(left_back), right[0], right[1], twiddle


def split(values):
    high = values.astype(jnp.bfloat16)
    low = (values - high.astype(jnp.float32)).astype(jnp.bfloat16)
    return high, low


def pair_kernel(rows, bands, windows, points, info, block, kernel, left, left_back, right, right_back,
                twiddle, out, projections, own, other, total):
    members = block.shape[0]
    piece = block.shape[3] // 2
    tall = members * piece
    quads = tall // points

    def load(orbital, part, h):
        value = block[:, orbital, part, h * piece:(h + 1) * piece, :]
        return value.astype(jnp.float32).reshape(tall, LANES)

    first_row = info[2 * windows]
    first_band = info[2 * windows + 1]
    for r in range(rows):
        for part in range(2):
            for h in range(2):
                own[r, part, h] = load(first_row + r, part, h)
    total[...] = jnp.zeros_like(total)

    def rotate(real_part, imag_part, p, sign):
        cos = twiddle[0, p * quads:(p + 1) * quads, :].reshape(quads, 1, LANES)
        sin = twiddle[1, p * quads:(p + 1) * quads, :].reshape(quads, 1, LANES) * sign
        real_part = real_part.reshape(quads, points, LANES)
        imag_part = imag_part.reshape(quads, points, LANES)
        new_real = real_part * cos - imag_part * sin
        new_imag = imag_part * cos + real_part * sin
        return new_real.reshape(tall, LANES), new_imag.reshape(tall, LANES)

    def dot(a, b):
        return jnp.dot(a, b, preferred_element_type=jnp.float32)

    def from_left(matrix, values):
        high, low = split(values)
        return dot(matrix, jnp.concatenate([high, high, low], axis=0))

    def from_right(values, matrix):
        high, low = split(values)
        return dot(jnp.concatenate([high, high, low], axis=1), matrix)

    def window_body(w, carry):
        slot = info[windows + w]

        def band_body(b, carry):
            orbital = w * bands + b
            for part in range(2):
                for h in range(2):
                    other[part, h] = load(orbital, part, h)
            inputs = ([], [])
            for r in range(rows):
                fields = []
                for h in range(2):
                    real_part = own[r, 0, h] * other[0, h] + own[r, 1, h] * other[1, h]
                    imag_part = own[r, 1, h] * other[0, h] - own[r, 0, h] * other[1, h]
                    fields.append(jnp.concatenate([real_part, imag_part], axis=0))
                inputs[0].append(fields[0] + fields[1])
                inputs[1].append(fields[0] - fields[1])
            turned = []
            for p in range(2):
                spectrum = from_left(left[p], jnp.concatenate(inputs[p], axis=1))
                for r in range(rows):
                    cut = spectrum[:, r * LANES:(r + 1) * LANES]
                    turned.append(jnp.concatenate(rotate(cut[:tall], cut[tall:], p, 1.0), axis=1))
            back = ([], [])
            for p in range(2):
                chosen = kernel[slot, p * tall:(p + 1) * tall, :]
                chosen = jnp.concatenate([chosen, chosen], axis=1)
                for r in range(rows):
                    full = from_right(turned[p * rows + r], right[...]) * chosen
                    full = from_right(full, right_back[...])
                    pair = rotate(full[:, :LANES], full[:, LANES:], p, -1.0)
                    back[p].append(jnp.concatenate(pair, axis=0))
            halves = [from_left(left_back[p], jnp.concatenate(back[p], axis=1)) for p in range(2)]
            for h in range(2):
                potential = halves[0] + halves[1] if h == 0 else halves[0] - halves[1]
                for r in range(rows):
                    real_part = potential[:tall, r * LANES:(r + 1) * LANES]
                    imag_part = potential[tall:, r * LANES:(r + 1) * LANES]
                    total[r, 0, h] += other[0, h] * real_part - other[1, h] * imag_part
                    total[r, 1, h] += other[0, h] * imag_part + other[1, h] * real_part
            return carry

        return lax.fori_loop(0, info[w], band_body, carry)

    lax.fori_loop(0, windows, window_body, 0)
    for r in range(rows):
        for part in range(2):
            for h in range(2):
                out[:, r, part, h * piece:(h + 1) * piece, :] = total[r, part, h].reshape(members, piece, LANES)

    def project(a, carry):
        for part in range(2):
            for h in range(2):
                other[part, h] = load(first_band + a, part, h)
        for r in range(rows):
            real_sum = jnp.zeros((tall, LANES), jnp.float32)
            imag_sum = jnp.zeros((tall, LANES), jnp.float32)
            for h in range(2):
                real_sum += other[0, h] * total[r, 0, h] + other[1, h] * total[r, 1, h]
                imag_sum += other[0, h] * total[r, 1, h] - other[1, h] * total[r, 0, h]
            projections[r, a] = jnp.concatenate(
                [jnp.sum(real_sum, axis=0, keepdims=True), jnp.sum(imag_sum, axis=0, keepdims=True)], axis=0)
        return carry

    lax.fori_loop(0, bands, project, 0)


def on_device(orbitals, band_counts, pair_slot, kernel):
    local, bands, _, planes, columns = orbitals.shape
    slots, points = kernel.shape[0], kernel.shape[1]
    members = lax.axis_size("ga")
    groups = lax.axis_size("ka")
    kpoints = local * groups
    group, member = lax.axis_index("ka"), lax.axis_index("ga")
    volume = float(points ** 3)
    wide = LANES // points
    quads = points // (2 * wide)
    tiles = columns // LANES
    rows = max(1, local * bands // members)
    share = max(1, members // (local * bands))
    windows = STEPS * local
    tables = build_tables(points, members)

    pieces = orbitals.reshape(local * bands, 2, planes, tiles, LANES).transpose(0, 1, 3, 2, 4)
    pieces = pieces.reshape(local * bands, 2, tiles * planes, LANES)
    blocks = [pieces]
    pairs = [(source, (source + 1) % groups) for source in range(groups)]
    for _ in range(STEPS - 1):
        blocks.append(lax.ppermute(blocks[-1], "ka", pairs))
    gathered = lax.all_gather(jnp.concatenate(blocks, axis=0), "ga", axis=0)

    whole = lax.all_gather(kernel, "ga", axis=2, tiled=True) * (-1.0 / (kpoints * volume))
    whole = whole.reshape(slots, points, wide, quads, 2, points).transpose(0, 4, 3, 1, 2, 5)
    whole = whole.reshape(slots, 2 * quads * points, LANES)

    first_row = member // share * rows
    own_kpoint = first_row // bands
    anchors = (group - jnp.arange(STEPS, dtype=jnp.int32)) % groups
    window = (anchors[:, None] * local + jnp.arange(local, dtype=jnp.int32)[None, :]).reshape(-1)
    slot_row = lax.dynamic_index_in_dim(pair_slot, group * local + own_kpoint, 0, keepdims=False)
    mine = jnp.arange(windows, dtype=jnp.int32) % share == member % share
    info = jnp.concatenate([jnp.where(mine, band_counts[window], 0), slot_row[window],
                            jnp.stack([first_row, own_kpoint * bands]).astype(jnp.int32)])

    tall = quads * points
    field = (rows, 2, 2, tall, LANES)
    smem = pl.BlockSpec(memory_space=pltpu.SMEM)
    vmem = pl.BlockSpec(memory_space=pltpu.VMEM)

    def body(*refs):
        pair_kernel(rows, bands, windows, points, *refs)

    spread, projections = pl.pallas_call(
        body,
        out_shape=(jax.ShapeDtypeStruct((members, rows, 2, tiles * planes, LANES), jnp.float32),
                   jax.ShapeDtypeStruct((rows, bands, 2, LANES), jnp.float32)),
        in_specs=[smem] + [vmem] * 7,
        out_specs=(vmem, vmem),
        scratch_shapes=[pltpu.VMEM(field, jnp.float32), pltpu.VMEM(field[1:], jnp.float32),
                        pltpu.VMEM(field, jnp.float32)],
        compiler_params=pltpu.CompilerParams(vmem_limit_bytes=48 * 2 ** 20),
        name="pairs",
    )(info, gathered, whole, *[jnp.asarray(table) for table in tables])

    copies = jnp.broadcast_to(projections.transpose(0, 2, 1, 3)[None], (members, rows, 2, bands, LANES))
    arrived = lax.all_to_all(jnp.concatenate([spread, copies], axis=3), "ga", split_axis=0, concat_axis=0, tiled=True)
    arrived = arrived.reshape(members * rows, 2, tiles * planes + bands, LANES)
    vectors = arrived[:, :, :tiles * planes]
    projections = arrived[:, :, tiles * planes:].reshape(local * bands, share, 2, bands, LANES).transpose(0, 1, 3, 2, 4)
    if share > 1:
        vectors = jnp.sum(vectors.reshape(local * bands, share, *vectors.shape[1:]), axis=1)
    vectors = vectors.reshape(local, bands, 2, tiles, planes, LANES).transpose(0, 1, 2, 4, 3, 5)
    vectors = vectors.reshape(local, bands, 2, planes, columns)
    sums = jnp.sum(jnp.sum(projections, axis=-1) / volume, axis=1)
    matrix = sums.reshape(local, bands, bands, 2).transpose(0, 3, 2, 1)
    own_counts = lax.dynamic_slice_in_dim(band_counts, group * local, local)
    occupied = (jnp.arange(bands)[None, :] < own_counts[:, None]).astype(jnp.float32)
    part = jnp.sum(occupied * jnp.diagonal(matrix[:, 0], axis1=1, axis2=2)) / (2.0 * kpoints)
    place = jnp.arange(groups, dtype=jnp.int32)
    terms = jnp.where(place == group, part, 0.0)
    for step in range(1, groups):
        ring = [(source, (source + step) % groups) for source in range(groups)]
        arrived = lax.ppermute(part.reshape(1), "ka", ring)
        terms = jnp.where(place == (group - step) % groups, arrived, terms)
    energy = jnp.sum(terms)
    return (vectors, matrix, energy)


def solution(mesh):
    in_specs = (P("ka", None, None, "ga", None), P(), P(), P(None, None, "ga"))
    out_specs = (P("ka", None, None, "ga", None), P("ka", None, None, None), P())
    return jax.shard_map(
        on_device, mesh=mesh, in_specs=in_specs, out_specs=out_specs, check_vma=False
    )
```

profile of v0, /device:TPU:0, one launch (start us, length us, event | category | flops | bytes accessed | tf_op | source)
XLA Modules:
  0.0 167.7 jit_solution(10427693084097187502)
XLA Ops:
  7.2 0.0 copy-start
  7.2 0.0 all-gather.4.cloned.1.call-start
  7.2 0.7 all-gather.4.cloned.1.call-update
  7.9 0.0 all-gather.6.cloned.1.call-start
  8.0 3.0 %collective-permute-start = (bf16[16,2,32,128]{3,2,1,0:T(8,128)(2,1)}, bf16[16,2,32,128]{3,2,1,0:T(8,128)(2,1)S(1)}, u32[]{:S(2)}, u32[]{:S(2)}) collective-permute-start(bf16[16,2,32,128]{3,2,1,0:T(8,128)(2,1)} %bitcast.50), channel_id=1, source_target_pairs={{0,8},{8,16},{16,24},{24,0},{1,9},{9,17},{17,25},{25,1},{2,10},{10... | collective-permute-start | bytes 786440 | tf_op jit(solution)/shard_map/ppermute | solution.py:187
  11.0 7.5 %collective-permute-done = bf16[16,2,32,128]{3,2,1,0:T(8,128)(2,1)S(1)} collective-permute-done((bf16[16,2,32,128]{3,2,1,0:T(8,128)(2,1)}, bf16[16,2,32,128]{3,2,1,0:T(8,128)(2,1)S(1)}, u32[]{:S(2)}, u32[]{:S(2)}) %collective-permute-start) | collective-permute-done | bytes 262176 | tf_op jit(solution)/shard_map/ppermute | solution.py:187
  18.5 1.8 %pad_maximum_fusion.1 = bf16[32,2,32,128]{3,2,1,0:T(8,128)(2,1)} fusion(bf16[16,2,32,128]{3,2,1,0:T(8,128)(2,1)S(1)} %collective-permute-done, bf16[16,2,32,128]{3,2,1,0:T(8,128)(2,1)} %bitcast.51), kind=kLoop, calls=%fused_computation.5 | loop fusion | flops 262144 | bytes 1048576 | tf_op jit(solution)/shard_map/concatenate | solution.py:188
  20.2 0.0 all-gather.6.cloned.1.call-update
  20.3 0.1 iota_add_fusion
  20.4 0.1 add.83
  20.5 0.0 copy-done
  20.5 0.6 gather_fusion.1
  21.1 1.3 gather_fusion
  22.4 0.1 pad_add_fusion.refs_0_
  22.5 13.7 %all-gather.4.cloned.1.call-done = f32[8,32,1024]{2,1,0:T(8,128)} async-done(((f32[8,32,128]{2,1,0:T(8,128)}), f32[8,32,1024]{2,1,0:T(8,128)}) %all-gather.4.cloned.1.call-update) | async-done | bytes 1048592 | tf_op jit(solution)/shard_map/all_gather | solution.py:190
  36.2 1.3 broadcast_multiply_fusion
  37.5 4.9 %reshape.92 = f32[8,32,4,4,2,32]{5,4,3,2,1,0:T(2,128)} reshape(f32[8,32,1024]{2,1,0:T(8,128)S(1)} %broadcast_multiply_fusion) | data formatting | bytes 2097152 | tf_op jit(solution)/shard_map/reshape | solution.py:191
  42.4 5.6 %copy.39 = f32[8,32,4,4,2,32]{5,2,1,3,4,0:T(4,128)} copy(f32[8,32,4,4,2,32]{5,4,3,2,1,0:T(2,128)} %reshape.92) | data formatting | bytes 2097152 | tf_op jit(solution)/shard_map/reshape | solution.py:191
  48.0 0.0 copy-start.1
  48.0 0.0 copy-start.2
  48.0 0.0 copy-start.3
  48.0 0.0 copy-start.5
  48.0 3.9 %reshape.93.refs_2_ = f32[8,256,128]{2,1,0:T(8,128)S(1)} reshape(f32[8,2,4,32,4,32]{5,4,3,2,1,0:T(4,128)} %bitcast.44) | data formatting | bytes 2097152 | tf_op jit(solution)/shard_map/reshape | solution.py:192
  51.9 32.1 %all-gather.6.cloned.1.call-done = bf16[256,2,32,128]{3,2,1,0:T(8,128)(2,1)} async-done(((bf16[32,2,32,128]{3,2,1,0:T(8,128)(2,1)}), bf16[256,2,32,128]{3,2,1,0:T(8,128)(2,1)}) %all-gather.6.cloned.1.call-update) | async-done | bytes 4194320 | tf_op jit(solution)/shard_map/all_gather | solution.py:188
  84.1 0.0 copy-done.1
  84.1 0.0 copy-done.2
  84.1 0.0 copy-done.3
  84.1 0.0 copy-done.4
  84.1 0.0 copy-done.5
  84.1 0.0 copy-start.6
  84.1 41.1 %pairs.1 = (f32[8,2,2,32,128]{4,3,2,1,0:T(8,128)S(1)}, f32[2,8,2,128]{3,2,1,0:T(2,128)S(1)}) custom-call(s32[10]{0:T(128)S(1)} %pad_add_fusion.refs_0_, bf16[8,32,2,32,128]{4,3,2,1,0:T(8,128)(2,1)} %bitcast.45, f32[8,256,128]{2,1,0:T(8,128)S(1)} %reshape.93.refs_2_, bf16[2,256,768]{2,1,0:T(8,128)(2,1)S(1)} %copy-done.1, bf16[2,256,768]{2,1,0:T(8,128)(2,1)S(1)} %copy-done.2, ...), custom_call_target="tpu_custom_call" | custom-call | tf_op jit(solution)/shard_map/pairs/pallas_call | solution.py:211
  125.2 0.9 pad_maximum_fusion
  126.1 3.5 %all-to-all-start = ((f32[8,2,2,40,128]{4,3,2,1,0:T(8,128)}), f32[8,2,2,40,128]{4,3,2,1,0:T(8,128)S(1)}, u32[]{:S(2)}, u32[]{:S(2)}) async-start(f32[8,2,2,40,128]{4,3,2,1,0:T(8,128)} %pad_maximum_fusion), calls=%async_computation | async-start | bytes 1310720 | tf_op jit(solution)/shard_map/all_to_all | solution.py:224
  129.7 0.0 copy-done.6
  129.7 0.1 dynamic_slice.8
  129.8 17.9 %all-to-all-done = f32[8,2,2,40,128]{4,3,2,1,0:T(8,128)S(1)} async-done(((f32[8,2,2,40,128]{4,3,2,1,0:T(8,128)}), f32[8,2,2,40,128]{4,3,2,1,0:T(8,128)S(1)}, u32[]{:S(2)}, u32[]{:S(2)}) %all-to-all-start) | async-done | bytes 655392 | tf_op jit(solution)/shard_map/all_to_all | solution.py:224
  147.7 0.1 slice_reduce_fusion
  147.8 0.1 copy.33
  147.9 0.1 copy.31
  148.0 0.6 gather_fusion.2
  148.6 0.6 fusion
  149.9 1.4 collective-permute-start.1
  151.2 2.7 %collective-permute-start.2 = (f32[1]{0:T(128)}, f32[1]{0:T(128)}, u32[]{:S(2)}, u32[]{:S(2)}) collective-permute-start(f32[1]{0:T(128)} %bitcast.25), channel_id=1, source_target_pairs={{0,16},{8,24},{16,0},{24,8},{1,17},{9,25},{17,1},{25,9},{2,18},{10... | collective-permute-start | bytes 20 | tf_op jit(solution)/shard_map/ppermute | solution.py:241
  153.9 2.0 %collective-permute-start.3 = (f32[1]{0:T(128)}, f32[1]{0:T(128)}, u32[]{:S(2)}, u32[]{:S(2)}) collective-permute-start(f32[1]{0:T(128)} %bitcast.25), channel_id=1, source_target_pairs={{0,8},{8,16},{16,24},{24,0},{1,9},{9,17},{17,25},{25,1},{2,10},{10... | collective-permute-start | bytes 20 | tf_op jit(solution)/shard_map/ppermute | solution.py:241
  155.9 1.0 reshape.96
  156.9 0.7 copy.32
  157.6 0.9 collective-permute-done.3
  158.5 2.4 %fusion.2 = f32[]{:T(128)} fusion(f32[]{:T(128)} %div.29, s32[]{:T(128)S(6)} %axis_index.23, f32[]{:T(128)} %bitcast.28, s32[]{:T(128)S(6)} %select_n.82, f32[]{:T(128)} %bitcast.27, s32[]{:T(128)S(6)} %select_n.81, f32[]{:T(128)} %bitcast.26, s32[]{:T(128)S(6)} %select_n.79), kind=kLoop, calls=%fused_computation.25 | loop fusion | flops 35 | bytes 36 | tf_op jit(solution)/shard_map/reduce_sum | solution.py:243
  (14 shorter events, 0.2 us)
Async XLA Ops:
  7.2 13.3 %copy-start = (s32[8,8]{1,0:T(8,128)S(1)}, s32[8,8]{1,0:T(8,128)}, u32[]{:S(2)}) copy-start(s32[8,8]{1,0:T(8,128)} %param.11) | copy-start | bytes 772
  7.2 29.0 %all-gather.4.cloned.1.call-start = ((), (), s32[]{:S(2)}) async-start(), calls=%async_computation.1 | async-start | bytes 1179648 | tf_op jit(solution)/shard_map/all_gather | solution.py:190
  7.9 76.1 %all-gather.6.cloned.1.call-start = ((), (), s32[]{:S(2)}) async-start(), calls=%async_computation.2 | async-start | bytes 4718592 | tf_op jit(solution)/shard_map/all_gather | solution.py:188
  8.0 10.5 %collective-permute-start = (bf16[16,2,32,128]{3,2,1,0:T(8,128)(2,1)}, bf16[16,2,32,128]{3,2,1,0:T(8,128)(2,1)S(1)}, u32[]{:S(2)}, u32[]{:S(2)}) collective-permute-start(bf16[16,2,32,128]{3,2,1,0:T(8,128)(2,1)} %bitcast.50), channel_id=1, source_target_pairs={{0,8},{8,16},{16,24},{24,0},{1,9},{9,17},{17,25},{25,1},{2,10},{10... | collective-permute-start | bytes 786440 | tf_op jit(solution)/shard_map/ppermute | solution.py:187
  48.0 36.1 %copy-start.1 = (bf16[2,256,768]{2,1,0:T(8,128)(2,1)S(1)}, bf16[2,256,768]{2,1,0:T(8,128)(2,1)}, u32[]{:S(2)}) copy-start(bf16[2,256,768]{2,1,0:T(8,128)(2,1)} %constant.122.clone.refs_3_) | copy-start | bytes 2359300
  48.0 36.1 %copy-start.2 = (bf16[2,256,768]{2,1,0:T(8,128)(2,1)S(1)}, bf16[2,256,768]{2,1,0:T(8,128)(2,1)}, u32[]{:S(2)}) copy-start(bf16[2,256,768]{2,1,0:T(8,128)(2,1)} %constant.123.clone.refs_4_) | copy-start | bytes 2359300
  48.0 36.1 %copy-start.3 = (bf16[768,256]{1,0:T(8,128)(2,1)S(1)}, bf16[768,256]{1,0:T(8,128)(2,1)}, u32[]{:S(2)}) copy-start(bf16[768,256]{1,0:T(8,128)(2,1)} %constant.124.clone.refs_5_) | copy-start | bytes 1179652
  48.0 36.1 %copy-start.4 = (bf16[768,256]{1,0:T(8,128)(2,1)S(1)}, bf16[768,256]{1,0:T(8,128)(2,1)}, u32[]{:S(2)}) copy-start(bf16[768,256]{1,0:T(8,128)(2,1)} %constant.125.clone.refs_6_) | copy-start | bytes 1179652
  48.0 36.1 %copy-start.5 = (f32[2,8,128]{2,1,0:T(8,128)S(1)}, f32[2,8,128]{2,1,0:T(8,128)}, u32[]{:S(2)}) copy-start(f32[2,8,128]{2,1,0:T(8,128)} %constant.126.clone.refs_7_) | copy-start | bytes 24580
  84.1 45.6 %copy-start.6 = (s32[8]{0:T(128)S(1)}, s32[8]{0:T(128)}, u32[]{:S(2)}) copy-start(s32[8]{0:T(128)} %param.10) | copy-start | bytes 100
  126.1 21.6 %all-to-all-start = ((f32[8,2,2,40,128]{4,3,2,1,0:T(8,128)}), f32[8,2,2,40,128]{4,3,2,1,0:T(8,128)S(1)}, u32[]{:S(2)}, u32[]{:S(2)}) async-start(f32[8,2,2,40,128]{4,3,2,1,0:T(8,128)} %pad_maximum_fusion), calls=%async_computation | async-start | bytes 1310720 | tf_op jit(solution)/shard_map/all_to_all | solution.py:224
  149.9 7.7 %collective-permute-start.1 = (f32[1]{0:T(128)}, f32[1]{0:T(128)}, u32[]{:S(2)}, u32[]{:S(2)}) collective-permute-start(f32[1]{0:T(128)} %bitcast.25), channel_id=1, source_target_pairs={{0,24},{8,0},{16,8},{24,16},{1,25},{9,1},{17,9},{25,17},{2,26},{10... | collective-permute-start | bytes 20 | tf_op jit(solution)/shard_map/ppermute | solution.py:241
  151.2 6.4 %collective-permute-start.2 = (f32[1]{0:T(128)}, f32[1]{0:T(128)}, u32[]{:S(2)}, u32[]{:S(2)}) collective-permute-start(f32[1]{0:T(128)} %bitcast.25), channel_id=1, source_target_pairs={{0,16},{8,24},{16,0},{24,8},{1,17},{9,25},{17,1},{25,9},{2,18},{10... | collective-permute-start | bytes 20 | tf_op jit(solution)/shard_map/ppermute | solution.py:241
  153.9 4.6 %collective-permute-start.3 = (f32[1]{0:T(128)}, f32[1]{0:T(128)}, u32[]{:S(2)}, u32[]{:S(2)}) collective-permute-start(f32[1]{0:T(128)} %bitcast.25), channel_id=1, source_target_pairs={{0,8},{8,16},{16,24},{24,0},{1,9},{9,17},{17,25},{25,1},{2,10},{10... | collective-permute-start | bytes 20 | tf_op jit(solution)/shard_map/ppermute | solution.py:241
Sparse Core Ops, SparseCore 0:
  9.6 26.5 all-gather.3
  38.4 45.6 all-gather.5
where the time goes:
time: 165 us; the launch traced here: 168 us
  waiting for transfers between devices  72.8 us (44%)
  Pallas kernels  41.1 us (25%)
  local copies, waits for them, and re-layouts  19 us (12%)
  between operations  14.9 us (9%)
  starting transfers between devices  12.6 us (8%)
  other arithmetic  7.33 us (4%)
    pallas_call x1, Pallas kernels, on_device(): pl.pallas_call(body, out_shape=(jax.ShapeDtypeStruct((members, rows, 2, t...  41.1 us
    all_gather x1, waiting for transfers between devices, on_device(): gathered = lax.all_gather(jnp.concatenate(blocks, axis=0), 'ga', axis=0)  32.1 us
    all_to_all x1, waiting for transfers between devices, on_device(): lax.all_to_all(jnp.concatenate([spread, copies], axis=3), 'ga', split_axi...  17.9 us
    all_gather x1, waiting for transfers between devices, on_device(): lax.all_gather(kernel, 'ga', axis=2, tiled=True)  13.7 us
    reshape x2, local copies, waits for them, and re-layouts, on_device(): whole.reshape(slots, points, wide, quads, 2, points)  10.5 us
    ppermute x1, waiting for transfers between devices, on_device(): blocks.append(lax.ppermute(blocks[-1], 'ka', pairs))  7.47 us
    ppermute x3, starting transfers between devices, on_device(): arrived = lax.ppermute(part.reshape(1), 'ka', ring)  5.97 us
    reshape x1, local copies, waits for them, and re-layouts, on_device(): whole = whole.reshape(slots, 2 * quads * points, LANES)  3.9 us
  transfers between devices with their start and end apart: 7, of which 5 were waited for; matrix products, arithmetic and copies ran while one was open for 13% of the time, Pallas kernels for 0%

commit v1 on v0

v1 whole, which is shorter than its diff:
```python
import functools

import jax
import jax.numpy as jnp
import numpy as np
from jax import lax
from jax.experimental import pallas as pl
from jax.experimental.pallas import tpu as pltpu
from jax.sharding import PartitionSpec as P

LANES = 128
CHUNK = 2
LAG = 5
MESH = pl.DeviceIdType.MESH


def split_np(matrix):
    high = matrix.astype(np.float32).astype(jnp.bfloat16)
    low = (matrix - high.astype(np.float64)).astype(np.float32).astype(jnp.bfloat16)
    return high, low


def real_form(matrix):
    return np.block([[matrix.real, -matrix.imag], [matrix.imag, matrix.real]])


def build_tables(points, members):
    wide = LANES // points
    quads = points // (2 * wide)
    planes = points // members
    dft = np.exp(-2j * np.pi * np.outer(np.arange(points), np.arange(points)) / points)
    member_of = np.arange(members).reshape(members // 2, 2).T.reshape(-1)
    x_of = (member_of[:, None] * planes + np.arange(planes)[None, :]).reshape(members, 1, planes)
    y1_of = np.arange(quads).reshape(1, quads, 1)
    x_of, y1_of = (np.broadcast_to(v, (members, quads, planes)).reshape(-1) for v in (x_of, y1_of))
    gx = np.tile(np.arange(points), quads)
    q = np.repeat(np.arange(quads), points)
    left, left_back = [], []
    for p in range(2):
        phase = np.outer(gx, x_of) / points + np.outer(p + 2 * q, y1_of) * wide / points
        forward = np.exp(-2j * np.pi * phase)
        high, low = split_np(real_form(forward))
        left.append(np.concatenate([high, low, high], axis=1))
        high, low = split_np(real_form(np.conj(forward).T))
        left_back.append(np.concatenate([high, low, high], axis=1))
    small = np.exp(-2j * np.pi * np.outer(np.arange(wide), np.arange(wide)) / wide)
    lane = np.kron(small, dft)
    right = []
    for matrix in (lane, np.conj(lane)):
        high, low = split_np(real_form(matrix).T)
        right.append(np.concatenate([high, low, high], axis=0))
    low_freq = (np.arange(2)[:, None] + 2 * np.arange(quads)[None, :]).reshape(-1)
    y0 = np.repeat(np.arange(wide), points)
    twiddle = np.exp(-2j * np.pi * np.outer(low_freq, y0) / points)
    twiddle = np.stack([twiddle.real, twiddle.imag]).astype(np.float32)
    return np.stack(left), np.stack(left_back), right[0], right[1], twiddle


def split(values):
    high = values.astype(jnp.bfloat16)
    low = (values - high.astype(jnp.float32)).astype(jnp.bfloat16)
    return high, low


def exchange_kernel(dims, counts, slots, pieces, kernel, left_in, left_back_in, right_in, right_back_in, twiddle_in,
                    out, matrix, energy,
                    block, left, left_back, right, right_back, twiddle, staged, raw, multiplier,
                    own, total, arrived, lanes_of, mail, mails, note, notes,
                    table_sem, local_sem, z_send, z_recv, d_send, d_recv, x_send, x_recv, p_send, p_recv,
                    kz_send, kz_recv, kd_send, kd_recv, o_send, o_recv, m_send, m_recv, e_send, e_recv):
    local, bands, members, groups, points, planes = dims
    orbitals = local * bands
    chips = members // 2
    rows = max(1, orbitals // members)
    share = max(1, members // orbitals)
    windows = 2 * local
    steps = orbitals // CHUNK
    wide = LANES // points
    quads = points // (2 * wide)
    tall = quads * points
    piece = tall // members
    held = points // members
    volume = float(points ** 3)
    scale = -1.0 / (groups * local * volume)
    ready = max(1, 2 * rows // CHUNK)

    me = lax.axis_index("ga")
    group = lax.axis_index("ka")
    core, chip = lax.rem(me, 2), lax.div(me, 2)
    partner = chip * 2 + 1 - core
    after = lax.rem(group + 1, groups)

    def row_of(member):
        return lax.div(member, share) * rows

    def start_of(at):
        return lax.div(row_of(at * 2), CHUNK)

    def chunk_of(at, j):
        return pl.ds(lax.rem(start_of(at) + j, steps) * CHUNK, CHUNK)

    first_row = row_of(me)
    own_local = lax.div(first_row, bands)
    window_kpoints = [lax.rem(group + groups - w // local, groups) * local + w % local for w in range(windows)]

    def remote(src, dst, send, recv, **where):
        return pltpu.make_async_remote_copy(src_ref=src, dst_ref=dst, send_sem=send, recv_sem=recv,
                                            device_id=where, device_id_type=MESH)

    table_copies = [pltpu.make_async_copy(src, dst, table_sem.at[i]) for i, (src, dst) in enumerate(
        [(left_in, left), (left_back_in, left_back), (right_in, right), (right_back_in, right_back),
         (twiddle_in, twiddle)])]
    for copy in table_copies:
        copy.start()
    place = pltpu.make_async_copy(pieces, block.at[pl.ds(0, orbitals), core, chip], local_sem.at[0])
    place.start()
    for l in range(local):
        for w in range(windows):
            staged[l, w] = kernel[slots[group * local + l, window_kpoints[w]]] * scale

    barrier = pltpu.get_barrier_semaphore()
    for d in range(1, members):
        pl.semaphore_signal(barrier, inc=1, device_id={"ga": lax.rem(me + d, members)}, device_id_type=MESH)
    for d in range(1, groups):
        pl.semaphore_signal(barrier, inc=1, device_id={"ka": lax.rem(group + d, groups)}, device_id_type=MESH)
    pl.semaphore_wait(barrier, members + groups - 2)

    def z_copy(j, d):
        at = lax.rem(chip + d, chips)
        chunk = chunk_of(at, j)
        return remote(pieces.at[chunk], block.at[chunk, core, chip], z_send.at[d - 1], z_recv.at[j], ga=at * 2 + core)

    def kz_copy(d):
        at = lax.rem(chip + d, chips)
        return remote(staged.at[lax.div(row_of(at * 2), bands)], raw.at[core, chip], kz_send.at[d - 1], kz_recv.at[0],
                      ga=at * 2 + core)

    for d in range(1, chips):
        kz_copy(d).start()

    def z_start(j, carry):
        for d in range(1, chips):
            z_copy(j, d).start()
        return carry

    lax.fori_loop(0, steps, z_start, 0)
    kplace = pltpu.make_async_copy(staged.at[own_local], raw.at[core, chip], local_sem.at[1])
    kplace.start()

    def d_copy(j):
        here = block.at[chunk_of(chip, j), core]
        return remote(here, here, d_send.at[j], d_recv.at[j], ga=partner)

    def x_copy(j):
        chunk = lax.rem(start_of(chip) + j, steps) * CHUNK
        return remote(block.at[pl.ds(chunk, CHUNK), core], block.at[pl.ds(orbitals + chunk, CHUNK), core],
                      x_send.at[j], x_recv.at[j], ka=after)

    def p_copy(j):
        chunk = lax.rem(start_of(chip) + j, steps) * CHUNK
        here = block.at[pl.ds(orbitals + chunk, CHUNK), core]
        return remote(here, here, p_send.at[j], p_recv.at[j], ga=partner)

    def wait_for(dst, sem):
        pltpu.make_async_copy(dst, dst, sem).wait()

    def pass_own(j):
        wait_for(block.at[pl.ds(0, CHUNK), 0, pl.ds(0, chips - 1)], z_recv.at[j])
        d_copy(j).start()
        x_copy(j).start()

    place.wait()
    kplace.wait()
    wait_for(raw.at[0, pl.ds(0, chips - 1)], kz_recv.at[0])
    kd_copy = remote(raw.at[core], raw.at[core], kd_send.at[0], kd_recv.at[0], ga=partner)
    kd_copy.start()
    for j in range(ready):
        pass_own(j)
    for copy in table_copies:
        copy.wait()
    total[...] = jnp.zeros_like(total)
    kd_copy.wait_recv()

    each = points // members
    for w in range(windows):
        for p in range(2):
            for q in range(quads):
                parts = []
                for a in range(wide):
                    gy = a * 2 * quads + 2 * q + p
                    at = gy // each
                    value = raw[at % 2, at // 2, w]
                    parts.append(value[:, (gy % each) * points:(gy % each + 1) * points])
                multiplier[w, (p * quads + q) * points:(p * quads + q + 1) * points, :] = jnp.concatenate(parts, axis=1)

    def load(slot, part, h):
        value = block[slot, :, :, part * 2 + h]
        return value.astype(jnp.float32).reshape(tall, LANES)

    for j in range(ready):
        d_copy(j).wait_recv()
    for r in range(rows):
        for part in range(2):
            for h in range(2):
                own[r, part, h] = load(first_row + r, part, h)

    def rotate(real_part, imag_part, p, sign):
        cos = twiddle[0, p * quads:(p + 1) * quads, :].reshape(quads, 1, LANES)
        sin = twiddle[1, p * quads:(p + 1) * quads, :].reshape(quads, 1, LANES) * sign
        real_part = real_part.reshape(quads, points, LANES)
        imag_part = imag_part.reshape(quads, points, LANES)
        new_real = real_part * cos - imag_part * sin
        new_imag = imag_part * cos + real_part * sin
        return new_real.reshape(tall, LANES), new_imag.reshape(tall, LANES)

    def dot(a, b):
        return jnp.dot(a, b, preferred_element_type=jnp.float32)

    def from_left(table, values):
        high, low = split(values)
        return dot(table, jnp.concatenate([high, high, low], axis=0))

    def from_right(values, table):
        high, low = split(values)
        return dot(jnp.concatenate([high, high, low], axis=1), table)

    def partner_body(i, carry):
        step = lax.div(i, CHUNK)
        fresh = lax.rem(i, CHUNK) == 0

        @pl.when(fresh & (step + ready < steps))
        def _():
            pass_own(step + ready)

        @pl.when(fresh & (step >= LAG) & (step < steps + LAG))
        def _():
            j = step - LAG
            x_copy(j).wait_recv()
            p_copy(j).start()

        @pl.when(fresh & (step >= ready) & (step < steps))
        def _():
            d_copy(step).wait_recv()

        @pl.when(fresh & (step >= steps))
        def _():
            p_copy(step - steps).wait_recv()

        back = lax.div(step, steps)
        orbital = lax.rem(start_of(chip) + lax.rem(step, steps), steps) * CHUNK + lax.rem(i, CHUNK)
        slot = back * orbitals + orbital
        at_local, band = lax.div(orbital, bands), lax.rem(orbital, bands)
        w = back * local + at_local
        kpoint = lax.rem(group + groups - back, groups) * local + at_local
        keep = jnp.where(band < counts[kpoint], 1.0, 0.0).astype(jnp.float32)
        if share > 1:
            keep = keep * jnp.where(lax.rem(w, share) == lax.rem(me, share), 1.0, 0.0).astype(jnp.float32)
        other = [[load(slot, part, h) * keep for h in range(2)] for part in range(2)]
        inputs = ([], [])
        for r in range(rows):
            fields = []
            for h in range(2):
                real_part = own[r, 0, h] * other[0][h] + own[r, 1, h] * other[1][h]
                imag_part = own[r, 1, h] * other[0][h] - own[r, 0, h] * other[1][h]
                fields.append(jnp.concatenate([real_part, imag_part], axis=0))
            inputs[0].append(fields[0] + fields[1])
            inputs[1].append(fields[0] - fields[1])
        turned = []
        for p in range(2):
            spectrum = from_left(left[p], jnp.concatenate(inputs[p], axis=1))
            for r in range(rows):
                cut = spectrum[:, r * LANES:(r + 1) * LANES]
                turned.append(jnp.concatenate(rotate(cut[:tall], cut[tall:], p, 1.0), axis=1))
        full = from_right(jnp.concatenate(turned, axis=0), right[...])
        weighted = []
        for p in range(2):
            chosen = multiplier[w, p * tall:(p + 1) * tall, :]
            chosen = jnp.concatenate([chosen, chosen], axis=1)
            for r in range(rows):
                n = p * rows + r
                weighted.append(full[n * tall:(n + 1) * tall] * chosen)
        full = from_right(jnp.concatenate(weighted, axis=0), right_back[...])
        halves = []
        for p in range(2):
            back_p = []
            for r in range(rows):
                n = p * rows + r
                cut = full[n * tall:(n + 1) * tall]
                back_p.append(jnp.concatenate(rotate(cut[:, :LANES], cut[:, LANES:], p, -1.0), axis=0))
            halves.append(from_left(left_back[p], jnp.concatenate(back_p, axis=1)))
        for h in range(2):
            potential = halves[0] + halves[1] if h == 0 else halves[0] - halves[1]
            for r in range(rows):
                real_part = potential[:tall, r * LANES:(r + 1) * LANES]
                imag_part = potential[tall:, r * LANES:(r + 1) * LANES]
                total[r, 0, h] += other[0][h] * real_part - other[1][h] * imag_part
                total[r, 1, h] += other[0][h] * imag_part + other[1][h] * real_part
        return carry

    lax.fori_loop(0, 2 * orbitals, partner_body, 0)

    def seat(member):
        return lax.rem(member, 2) * chips + lax.div(member, 2)

    def o_copy(d):
        to = lax.rem(me + d, members)
        return remote(total.at[:, :, :, pl.ds(pl.multiple_of(seat(to) * piece, piece), piece)],
                      arrived.at[lax.rem(me, share), pl.ds(first_row, rows)], o_send.at[d - 1], o_recv.at[d - 1], ga=to)

    for d in range(1, members):
        o_copy(d).start()

    def project(a, carry):
        for r in range(rows):
            real_sum = jnp.zeros((tall, LANES), jnp.float32)
            imag_sum = jnp.zeros((tall, LANES), jnp.float32)
            for h in range(2):
                first, second = load(own_local * bands + a, 0, h), load(own_local * bands + a, 1, h)
                real_sum += first * total[r, 0, h] + second * total[r, 1, h]
                imag_sum += first * total[r, 1, h] - second * total[r, 0, h]
            lanes_of[r, 0, pl.ds(a, 1)] = jnp.sum(real_sum, axis=0, keepdims=True)
            lanes_of[r, 1, pl.ds(a, 1)] = jnp.sum(imag_sum, axis=0, keepdims=True)
        return carry

    lax.fori_loop(0, bands, project, 0)
    lane = lax.broadcasted_iota(jnp.int32, (bands, LANES), 1)
    level = lax.broadcasted_iota(jnp.int32, (bands, LANES), 0)
    entry = 2 * local * bands
    letter = jnp.zeros((bands, LANES), jnp.float32)
    for r in range(rows):
        at_band = lax.rem(first_row, bands) + r
        filled = jnp.where(at_band < counts[group * local + own_local], 1.0, 0.0).astype(jnp.float32)
        for part in range(2):
            value = jnp.sum(lanes_of[r, part], axis=1, keepdims=True) / volume
            letter = jnp.where(lane == (own_local * 2 + part) * bands + at_band, value, letter)
            if part == 0:
                term = jnp.where(level == at_band, value, 0.0) * (filled / (2.0 * groups * local))
                letter = letter + jnp.where(lane == entry, term, 0.0)
    mail[...] = letter
    mails[me] = letter

    def m_copy(d):
        to = lax.rem(me + d, members)
        return remote(mail, mails.at[me], m_send.at[d - 1], m_recv.at[d - 1], ga=to)

    for d in range(1, members):
        m_copy(d).start()

    own_part = pltpu.make_async_copy(total.at[:, :, :, pl.ds(pl.multiple_of(seat(me) * piece, piece), piece)],
                                     arrived.at[lax.rem(me, share), pl.ds(first_row, rows)], local_sem.at[2])
    own_part.start()
    for d in range(1, members):
        m_copy(d).wait_recv()
    summed = jnp.sum(mails[...], axis=0)
    for l in range(local):
        for part in range(2):
            begin = (l * 2 + part) * bands
            matrix[l, part] = summed[:, begin:begin + bands]
    mine = jnp.where(lane == entry, summed, 0.0)
    note[...] = mine
    notes[group] = mine

    def e_copy(d):
        to = lax.rem(group + d, groups)
        return remote(note, notes.at[group], e_send.at[d - 1], e_recv.at[d - 1], ka=to)

    for d in range(1, groups):
        e_copy(d).start()

    own_part.wait()
    for d in range(1, members):
        o_copy(d).wait_recv()

    def place_out(o, carry):
        l, b = lax.div(o, bands), lax.rem(o, bands)
        for part in range(2):
            for h in range(2):
                value = arrived[0, o, part, h]
                for n in range(1, share):
                    value = value + arrived[n, o, part, h]
                for y in range(quads):
                    t = h * quads + y
                    out[l, b, part, :, t * LANES:(t + 1) * LANES] = value[y * held:(y + 1) * held]
        return carry

    lax.fori_loop(0, orbitals, place_out, 0)
    for d in range(1, groups):
        e_copy(d).wait_recv()
    energy[0, 0] = jnp.sum(notes[...])

    for d in range(1, chips):
        wait_for(pieces, z_send.at[d - 1])
        kz_copy(d).wait_send()
    kd_copy.wait_send()

    def drain(j, carry):
        d_copy(j).wait_send()
        x_copy(j).wait_send()
        p_copy(j).wait_send()
        return carry

    lax.fori_loop(0, steps, drain, 0)
    for d in range(1, members):
        o_copy(d).wait_send()
        m_copy(d).wait_send()
    for d in range(1, groups):
        e_copy(d).wait_send()


def on_device(orbitals, band_counts, pair_slot, kernel):
    local, bands, _, planes, columns = orbitals.shape
    slots, points, width = kernel.shape
    members = lax.axis_size("ga")
    groups = lax.axis_size("ka")
    wide = LANES // points
    quads = points // (2 * wide)
    tall = quads * points
    tiles = columns // LANES
    count = local * bands
    rows = max(1, count // members)
    share = max(1, members // count)
    windows = 2 * local
    piece = tall // members
    steps = count // CHUNK
    chips = members // 2
    tables = build_tables(points, members)
    f32, bf16 = jnp.float32, jnp.bfloat16

    pieces = orbitals.reshape(count, 2, planes, tiles, LANES).transpose(0, 1, 3, 2, 4)
    pieces = pieces.reshape(count, 4, piece, LANES)

    smem = pl.BlockSpec(memory_space=pltpu.SMEM)
    vmem = pl.BlockSpec(memory_space=pltpu.VMEM)
    anywhere = pl.BlockSpec(memory_space=pl.ANY)
    dims = (local, bands, members, groups, points, planes)
    dma = pltpu.SemaphoreType.DMA
    out, matrix, energy = pl.pallas_call(
        functools.partial(exchange_kernel, dims),
        out_shape=(jax.ShapeDtypeStruct((local, bands, 2, planes, columns), f32),
                   jax.ShapeDtypeStruct((local, 2, bands, bands), f32),
                   jax.ShapeDtypeStruct((1, 1), f32)),
        in_specs=[smem, smem, vmem, vmem] + [anywhere] * 5,
        out_specs=(vmem, vmem, smem),
        scratch_shapes=[
            pltpu.VMEM((2 * count, 2, chips, 4, piece, LANES), bf16),
            pltpu.VMEM(tables[0].shape, bf16), pltpu.VMEM(tables[1].shape, bf16),
            pltpu.VMEM(tables[2].shape, bf16), pltpu.VMEM(tables[3].shape, bf16),
            pltpu.VMEM(tables[4].shape, f32),
            pltpu.VMEM((local, windows, points, width), f32),
            pltpu.VMEM((2, chips, windows, points, width), f32),
            pltpu.VMEM((windows, 2 * tall, LANES), f32),
            pltpu.VMEM((rows, 2, 2, tall, LANES), f32),
            pltpu.VMEM((rows, 2, 2, tall, LANES), f32),
            pltpu.VMEM((share, count, 2, 2, piece, LANES), f32),
            pltpu.VMEM((rows, 2, bands, LANES), f32),
            pltpu.VMEM((bands, LANES), f32),
            pltpu.VMEM((members, bands, LANES), f32),
            pltpu.VMEM((bands, LANES), f32),
            pltpu.VMEM((groups, bands, LANES), f32),
            dma((5,)), dma((3,)),
            dma((chips - 1,)), dma((steps,)), dma((steps,)), dma((steps,)), dma((steps,)), dma((steps,)),
            dma((steps,)), dma((steps,)),
            dma((chips - 1,)), dma((1,)), dma((1,)), dma((1,)),
            dma((members - 1,)), dma((members - 1,)), dma((members - 1,)), dma((members - 1,)),
            dma((groups - 1,)), dma((groups - 1,)),
        ],
        compiler_params=pltpu.CompilerParams(vmem_limit_bytes=56 * 2 ** 20, collective_id=0, has_side_effects=True),
        name="exchange",
    )(band_counts, pair_slot, pieces, kernel, *[jnp.asarray(table) for table in tables])
    return out, matrix, energy.reshape(())


def solution(mesh):
    in_specs = (P("ka", None, None, "ga", None), P(), P(), P(None, None, "ga"))
    out_specs = (P("ka", None, None, "ga", None), P("ka", None, None, None), P())
    return jax.shard_map(
        on_device, mesh=mesh, in_specs=in_specs, out_specs=out_specs, check_vma=False
    )
```

time: 165 us -> 108 us (0.65)
  the two profiles are of different devices: /device:TPU:0 before, /device:TPU:16 now
where the time goes in v1:
time: 108 us
  Pallas kernels  103 us (95%)
  local copies, waits for them, and re-layouts  2.5 us (2%)
  between operations  2.38 us (2%)
    pallas_call x1, Pallas kernels, on_device(): pl.pallas_call(functools.partial(exchange_kernel, dims), out_shape=(jax.S...  103 us
    unnamed x4, local copies, waits for them, and re-layouts  2.5 us

profile of v1, /device:TPU:16, one launch (start us, length us, event | category | flops | bytes accessed | tf_op | source)
XLA Modules:
  0.0 108.2 jit_solution(9674385217513568447)
XLA Ops:
  0.6 103.3 %exchange.1 = (f32[2,8,2,4,1024]{4,3,2,1,0:T(4,128)}, f32[2,2,8,8]{3,2,1,0:T(8,128)}, f32[1,1]{1,0:T(1,128)}) custom-call(s32[8]{0:T(128)} %counts.1, s32[8,8]{1,0:T(8,128)} %slots.1, bf16[16,4,16,128]{3,2,1,0:T(8,128)(2,1)} %bitcast.6, f32[8,32,128]{2,1,0:T(8,128)} %kernel.1, bf16[2,256,768]{2,1,0:T(8,128)(2,1)} %constant.10.clone.left_in, ...), custom_call_target="tpu_custom_call" | custom-call | tf_op jit(solution)/shard_map/exchange/pallas_call | solution.py:437
  104.0 0.0 copy-start
  104.0 1.9 %copy.16 = f32[2,8,2,4,1024]{4,3,2,1,0:T(4,128)} copy(f32[2,8,2,4,1024]{4,3,2,1,0:T(4,128)} %get-tuple-element.12) | data formatting | bytes 1048576
  105.9 0.0 copy-done
  105.9 0.6 copy.17
Async XLA Ops:
  104.0 1.9 %copy-start = (f32[2,2,8,8]{3,2,1,0:T(8,128)S(1)}, f32[2,2,8,8]{3,2,1,0:T(8,128)}, u32[]{:S(2)}) copy-start(f32[2,2,8,8]{3,2,1,0:T(8,128)} %get-tuple-element.13) | copy-start | bytes 3076

commit v2 on v1

v2 whole, which is shorter than its diff:
```python
import functools

import jax
import jax.numpy as jnp
import numpy as np
from jax import lax
from jax.experimental import pallas as pl
from jax.experimental.pallas import tpu as pltpu
from jax.sharding import PartitionSpec as P

LANES = 128
RADIX = 4
CHUNK = 2
LEAD = 3
SPLIT = 6
MESH = pl.DeviceIdType.MESH


def split_np(matrix):
    high = matrix.astype(np.float32).astype(jnp.bfloat16)
    low = (matrix - high.astype(np.float64)).astype(np.float32).astype(jnp.bfloat16)
    return high, low


def real_form(matrix):
    return np.block([[matrix.real, -matrix.imag], [matrix.imag, matrix.real]])


def build_tables(points, members):
    wide = LANES // points
    quads = points // (2 * wide)
    planes = points // members
    dft = np.exp(-2j * np.pi * np.outer(np.arange(points), np.arange(points)) / points)
    member_of = np.arange(members).reshape(members // 2, 2).T.reshape(-1)
    x_of = (member_of[:, None] * planes + np.arange(planes)[None, :]).reshape(members, 1, planes)
    deep = 2 * quads // RADIX
    b_of = np.arange(deep).reshape(1, deep, 1)
    x_of, b_of = (np.broadcast_to(v, (members, deep, planes)).reshape(-1) for v in (x_of, b_of))
    gx = np.tile(np.arange(points), deep)
    high_freq = np.repeat(np.arange(deep), points)
    left, left_back = [], []
    for c in range(RADIX):
        phase = np.outer(gx, x_of) / points + np.outer(c + RADIX * high_freq, b_of) / (2 * quads)
        forward = np.exp(-2j * np.pi * phase)
        high, low = split_np(real_form(forward))
        left.append(np.concatenate([high, high, low], axis=1))
        high, low = split_np(real_form(np.conj(forward).T))
        left_back.append(np.concatenate([high, high, low], axis=1))
    small = np.exp(-2j * np.pi * np.outer(np.arange(wide), np.arange(wide)) / wide)
    lane = np.kron(small, dft)
    right = []
    for matrix in (lane, np.conj(lane)):
        high, low = split_np(real_form(matrix).T)
        right.append(np.concatenate([high, low, high], axis=0))
    low_freq = (np.arange(RADIX)[:, None] + RADIX * np.arange(deep)[None, :]).reshape(-1)
    y0 = np.repeat(np.arange(wide), points)
    twiddle = np.exp(-2j * np.pi * np.outer(low_freq, y0) / points)
    twiddle = np.stack([twiddle.real, twiddle.imag]).astype(np.float32)
    return np.stack(left), np.stack(left_back), right[0], right[1], twiddle


def split(values):
    high = values.astype(jnp.bfloat16)
    low = (values - high.astype(jnp.float32)).astype(jnp.bfloat16)
    return high, low


def exchange_kernel(dims, counts, slots, pieces, kernel, left_in, left_back_in, right_in, right_back_in, twiddle_in,
                    out, matrix, energy,
                    block, left, left_back, right, right_back, twiddle, staged, raw, multiplier,
                    own, total, arrived, lanes_of, mail, mails, note, notes,
                    table_sem, local_sem, z_send, z_recv, r_send, d_send, d_recv, xo_send, xo_recv, x_send, x_recv,
                    p_send, p_recv, kz_send, kz_recv, kd_send, kd_recv, o_send, o_recv, m_send, m_recv, e_send, e_recv):
    local, bands, members, groups, points, planes = dims
    orbitals = local * bands
    chips = members // 2
    rows = max(1, orbitals // members)
    share = max(1, members // orbitals)
    landing = out if share == 1 else arrived
    windows = 2 * local
    steps = orbitals // CHUNK
    wide = LANES // points
    quads = points // (2 * wide)
    tall = quads * points
    deep = 2 * quads // RADIX
    low = deep * points
    piece = tall // members
    held = points // members
    volume = float(points ** 3)
    scale = -1.0 / (groups * local * volume)
    ready = max(1, 2 * rows // CHUNK)
    lead = min(max(LEAD, ready), steps)
    late = SPLIT if rows > 1 else 0
    paired = steps - max(late, lead)
    turns = 2 * steps - late
    relayed = 2 < chips <= 4

    me = lax.axis_index("ga")
    group = lax.axis_index("ka")
    core, chip = lax.rem(me, 2), lax.div(me, 2)
    partner = chip * 2 + 1 - core
    after = lax.rem(group + 1, groups)

    def row_of(member):
        return lax.div(member, share) * rows

    def start_of(at):
        return lax.div(row_of(at * 2), CHUNK)

    def chunk_at(at, j):
        rising = lax.rem(start_of(at) + j, steps)
        falling = lax.rem(start_of(at) + ready - 1 - j + 2 * steps, steps)
        return jnp.where(at < chips // 2, rising, falling) * CHUNK

    def chunk_of(at, j):
        return pl.ds(chunk_at(at, j), CHUNK)

    first_row = row_of(me)
    own_local = lax.div(first_row, bands)
    window_kpoints = [lax.rem(group + groups - w // local, groups) * local + w % local for w in range(windows)]

    def remote(src, dst, send, recv, **where):
        return pltpu.make_async_remote_copy(src_ref=src, dst_ref=dst, send_sem=send, recv_sem=recv,
                                            device_id=where, device_id_type=MESH)

    table_copies = [pltpu.make_async_copy(src, dst, table_sem.at[i]) for i, (src, dst) in enumerate(
        [(left_in, left), (left_back_in, left_back), (right_in, right), (right_back_in, right_back),
         (twiddle_in, twiddle)])]
    for copy in table_copies:
        copy.start()
    place = pltpu.make_async_copy(pieces, block.at[pl.ds(0, orbitals), core, chip], local_sem.at[0])
    place.start()
    for l in range(local):
        for w in range(windows):
            staged[l, w] = kernel[slots[group * local + l, window_kpoints[w]]] * scale

    barrier = pltpu.get_barrier_semaphore()
    for d in range(1, members):
        pl.semaphore_signal(barrier, inc=1, device_id={"ga": lax.rem(me + d, members)}, device_id_type=MESH)
    for d in range(1, groups):
        pl.semaphore_signal(barrier, inc=1, device_id={"ka": lax.rem(group + d, groups)}, device_id_type=MESH)
    pl.semaphore_wait(barrier, members + groups - 2)

    offsets = [d for d in range(1 - chips, chips) if d != 0]
    ordered = sorted(offsets, key=lambda d: -abs(d))

    def z_copy(j, d):
        chunk = chunk_of(chip + d, j)
        return remote(pieces.at[chunk], block.at[chunk, core, chip], z_send.at[offsets.index(d)], z_recv.at[j],
                      ga=(chip + d) * 2 + core)

    def inside(d):
        return (chip + d >= 0) & (chip + d < chips)

    def far(d):
        return relayed and abs(d) == chips - 1

    def z_start(j, stop):
        for d in ordered:
            @pl.when(inside(d) & (j < (ready if far(d) else steps)))
            def _():
                z_copy(j, d).start()
        return stop

    def kz_copy(half, d):
        at = lax.rem(chip + d, chips)
        part = pl.ds(half * local, local)
        return remote(staged.at[lax.div(row_of(at * 2), bands), part], raw.at[half, core, chip],
                      kz_send.at[half, d - 1], kz_recv.at[half], ga=at * 2 + core)

    def relay_copy(j):
        low = chip == 1
        end, origin = jnp.where(low, 0, chips - 1), jnp.where(low, chips - 1, 0)
        chunk = chunk_of(end, j)
        here = block.at[chunk, core, origin]
        return remote(here, here, r_send.at[0], z_recv.at[j], ga=end * 2 + core)

    xo_copy = remote(pieces, block.at[pl.ds(orbitals, orbitals), core, chip], xo_send.at[0], xo_recv.at[0], ka=after)
    for j in range(ready):
        z_start(j, 0)
    for d in range(1, chips):
        kz_copy(0, d).start()
    xo_copy.start()
    for j in range(ready, lead):
        z_start(j, 0)
    for d in range(1, chips):
        kz_copy(1, d).start()
    lax.fori_loop(lead, steps, z_start, 0)
    kplaces = [pltpu.make_async_copy(staged.at[own_local, pl.ds(half * local, local)], raw.at[half, core, chip],
                                     local_sem.at[1 + half]) for half in range(2)]
    for copy in kplaces:
        copy.start()

    def d_copy(j):
        here = block.at[chunk_of(chip, j), core]
        return remote(here, here, d_send.at[j], d_recv.at[j], ga=partner)

    def x_copy(j, d):
        chunk = chunk_at(chip, j)
        at = lax.rem(chip + d, chips)
        return remote(block.at[pl.ds(chunk, CHUNK), core, at], block.at[pl.ds(orbitals + chunk, CHUNK), core, at],
                      x_send.at[d - 1], x_recv.at[j], ka=after)

    def p_copy(j):
        chunk = chunk_at(chip, j)
        here = block.at[pl.ds(orbitals + chunk, CHUNK), core]
        return remote(here, here, p_send.at[j], p_recv.at[j], ga=partner)

    def wait_for(dst, sem):
        pltpu.make_async_copy(dst, dst, sem).wait()

    def arrived_z(sem):
        wait_for(block.at[pl.ds(0, CHUNK), 0, pl.ds(0, chips - 1)], sem)

    def pass_own(j):
        arrived_z(z_recv.at[j])
        if relayed:
            @pl.when(((chip == 1) | (chip == chips - 2)) & (j + ready < steps))
            def _():
                relay_copy(j + ready).start()
        d_copy(j).start()
        for d in range(1, chips):
            x_copy(j, d).start()

    def kd_copy(half):
        return remote(raw.at[half, core], raw.at[half, core], kd_send.at[half], kd_recv.at[half], ga=partner)

    def pass_kernel(half):
        kplaces[half].wait()
        wait_for(raw.at[half, 0, pl.ds(0, chips - 1)], kz_recv.at[half])
        kd_copy(half).start()

    place.wait()
    for j in range(ready):
        pass_own(j)
    pass_kernel(0)
    for copy in table_copies:
        copy.wait()
    total[...] = jnp.zeros_like(total)

    each = points // members

    def lay_out(half):
        kd_copy(half).wait_recv()
        for l in range(local):
            for c in range(RADIX):
                for q in range(deep):
                    parts = []
                    for a in range(wide):
                        gy = a * 2 * quads + c + RADIX * q
                        at = gy // each
                        value = raw[half, at % 2, at // 2, l]
                        parts.append(value[:, (gy % each) * points:(gy % each + 1) * points])
                    multiplier[half * local + l, (c * deep + q) * points:(c * deep + q + 1) * points, :] = (
                        jnp.concatenate(parts, axis=1))

    lay_out(0)

    def load(slot, part, h):
        value = block[slot, :, :, part * 2 + h]
        return value.astype(jnp.float32).reshape(tall, LANES)

    for j in range(ready):
        d_copy(j).wait_recv()
    for r in range(rows):
        for part in range(2):
            for h in range(2):
                own[r, part, h] = load(first_row + r, part, h)

    def rotate(real_part, imag_part, c, sign):
        cos = twiddle[0, c * deep:(c + 1) * deep, :].reshape(deep, 1, LANES)
        sin = twiddle[1, c * deep:(c + 1) * deep, :].reshape(deep, 1, LANES) * sign
        real_part = real_part.reshape(deep, points, LANES)
        imag_part = imag_part.reshape(deep, points, LANES)
        new_real = real_part * cos - imag_part * sin
        new_imag = imag_part * cos + real_part * sin
        return new_real.reshape(low, LANES), new_imag.reshape(low, LANES)

    def quarters(value):
        value = value.reshape(members, 2, piece // 2, LANES)
        return [value[:, n].reshape(low, LANES) for n in range(2)]

    def joined(first, second):
        shape = (members, 1, piece // 2, LANES)
        return jnp.concatenate([first.reshape(shape), second.reshape(shape)], axis=1).reshape(tall, LANES)

    def dot(a, b):
        return jnp.dot(a, b, preferred_element_type=jnp.float32)

    def from_left(table, values):
        high, low = split(values)
        return dot(table, jnp.concatenate([high, low, high], axis=0))

    def from_right(values, table):
        high, low = split(values)
        return dot(jnp.concatenate([high, high, low], axis=1), table)

    def turn_of(t):
        u = t - lead
        middle = (u >= 0) & (u < 2 * paired)
        back = jnp.where(middle, 1 - lax.rem(jnp.maximum(u, 0), 2), jnp.where(t - paired < steps, 0, 1))
        half = lax.div(jnp.maximum(u, 0), 2)
        index = jnp.where(u < 0, t, jnp.where(middle, jnp.where(back == 1, half, lead + half),
                                              jnp.where(t - paired < steps, t - paired, t - steps)))
        return back, index

    def partner_of(back, index, i):
        orbital = chunk_at(chip, index) + i
        slot = back * orbitals + orbital
        at_local, band = lax.div(orbital, bands), lax.rem(orbital, bands)
        w = back * local + at_local
        kpoint = lax.rem(group + groups - back, groups) * local + at_local
        keep = jnp.where(band < counts[kpoint], 1.0, 0.0).astype(jnp.float32)
        if share > 1:
            keep = keep * jnp.where(lax.rem(w, share) == lax.rem(me, share), 1.0, 0.0).astype(jnp.float32)
        return slot, w, keep

    def loads(item):
        held_ = {}
        for (slot, _, _), _ in item:
            if id(slot) not in held_:
                held_[id(slot)] = [[load(slot, part, h) for h in range(2)] for part in range(2)]
        return [held_[id(slot)] for (slot, _, _), _ in item]

    def first_stage(item):
        inputs = [[] for _ in range(RADIX)]
        for other, (_, r) in zip(loads(item), item):
            real, imag = [], []
            for h in range(2):
                real += quarters(own[r, 0, h] * other[0][h] + own[r, 1, h] * other[1][h])
                imag += quarters(own[r, 1, h] * other[0][h] - own[r, 0, h] * other[1][h])
            even = [[v[0] + v[2], v[1] + v[3]] for v in (real, imag)]
            odd = [[v[0] - v[2], v[1] - v[3]] for v in (real, imag)]
            inputs[0].append(jnp.concatenate([even[0][0] + even[0][1], even[1][0] + even[1][1]], axis=0))
            inputs[2].append(jnp.concatenate([even[0][0] - even[0][1], even[1][0] - even[1][1]], axis=0))
            inputs[1].append(jnp.concatenate([odd[0][0] + odd[1][1], odd[1][0] - odd[0][1]], axis=0))
            inputs[3].append(jnp.concatenate([odd[0][0] - odd[1][1], odd[1][0] + odd[0][1]], axis=0))
        return [from_left(left[c], jnp.concatenate(inputs[c], axis=1)) for c in range(RADIX)]

    def second_stage(spectra):
        result = []
        for p in range(2):
            turned = []
            for c in range(p * RADIX // 2, (p + 1) * RADIX // 2):
                for n in range(spectra[c].shape[1] // LANES):
                    cut = spectra[c][:, n * LANES:(n + 1) * LANES]
                    turned.append(jnp.concatenate(rotate(cut[:low], cut[low:], c, 1.0), axis=1))
            result.append(from_right(jnp.concatenate(turned, axis=0), right[...]))
        return result

    def third_stage(item, full):
        result = []
        for p in range(2):
            weighted = []
            for n in range(RADIX // 2):
                c = p * RADIX // 2 + n
                chosen = {}
                for i, ((slot, w, keep), _) in enumerate(item):
                    if id(slot) not in chosen:
                        value = multiplier[w, c * low:(c + 1) * low, :] * keep
                        chosen[id(slot)] = jnp.concatenate([value, value], axis=1)
                    at = n * len(item) + i
                    weighted.append(full[p][at * low:(at + 1) * low] * chosen[id(slot)])
            result.append(from_right(jnp.concatenate(weighted, axis=0), right_back[...]))
        return result

    def fourth_stage(item, full):
        values = []
        for p in range(2):
            for n in range(RADIX // 2):
                c = p * RADIX // 2 + n
                back_c = []
                for i in range(len(item)):
                    at = n * len(item) + i
                    cut = full[p][at * low:(at + 1) * low]
                    back_c.append(jnp.concatenate(rotate(cut[:, :LANES], cut[:, LANES:], c, -1.0), axis=0))
                values.append(from_left(left_back[c], jnp.concatenate(back_c, axis=1)))
        return values

    def last_stage(item, values):
        for i, (other, (_, r)) in enumerate(zip(loads(item), item)):
            cut = [value[:, i * LANES:(i + 1) * LANES] for value in values]
            real, imag = [v[:low] for v in cut], [v[low:] for v in cut]
            even = [[v[0] + v[2], v[1] + v[3]] for v in (real, imag)]
            odd = [[v[0] - v[2], v[1] - v[3]] for v in (real, imag)]
            real = [even[0][0] + even[0][1], odd[0][0] - odd[1][1], even[0][0] - even[0][1], odd[0][0] + odd[1][1]]
            imag = [even[1][0] + even[1][1], odd[1][0] + odd[0][1], even[1][0] - even[1][1], odd[1][0] - odd[0][1]]
            for h in range(2):
                real_part = joined(real[2 * h], real[2 * h + 1])
                imag_part = joined(imag[2 * h], imag[2 * h + 1])
                total[r, 0, h] += other[0][h] * real_part - other[1][h] * imag_part
                total[r, 1, h] += other[0][h] * imag_part + other[1][h] * real_part

    def work(a, b):
        va = first_stage(a)
        vb = first_stage(b)
        va = second_stage(va)
        vb = second_stage(vb)
        va = third_stage(a, va)
        vb = third_stage(b, vb)
        va = fourth_stage(a, va)
        vb = fourth_stage(b, vb)
        last_stage(a, va)
        last_stage(b, vb)

    def pass_back(j):
        wait_for(block.at[pl.ds(0, CHUNK), 0, pl.ds(0, chips - 1)], x_recv.at[j])
        p_copy(j).start()

    def step_body(step, carry):
        back, index = turn_of(step)
        next_back, next_index = turn_of(step + 1)

        @pl.when((next_back == 0) & (next_index >= ready))
        def _():
            pass_own(next_index)

        @pl.when(step == lead - 1)
        def _():
            xo_copy.wait_recv()
            pass_kernel(1)

        @pl.when((next_back == 1) & (step + 1 < turns))
        def _():
            pass_back(next_index)

        if late:
            @pl.when((step >= turns - late + 1) & (step + 1 < turns + late))
            def _():
                pass_back(step - turns + late - 1 + steps - late)

        @pl.when((back == 0) & (index >= ready))
        def _():
            d_copy(index).wait_recv()

        @pl.when(step == lead)
        def _():
            lay_out(1)

        @pl.when(back == 1)
        def _():
            p_copy(index).wait_recv()

        partners = [partner_of(back, index, i) for i in range(CHUNK)]
        work(*[[(partner, r) for r in range(rows)] for partner in partners])
        return carry

    lax.fori_loop(0, turns, step_body, 0)

    def seat(member):
        return lax.rem(member, 2) * chips + lax.div(member, 2)

    def o_copy(d, r):
        to = lax.rem(me + d, members)
        return remote(total.at[r, :, :, pl.ds(pl.multiple_of(seat(to) * piece, piece), piece)],
                      landing.at[lax.rem(me, share) * orbitals + first_row + r], o_send.at[r, d - 1], o_recv.at[r, d - 1],
                      ga=to)

    if late:
        pass_back(steps - 1)

    def row_body(r, carry):
        def turn(q, carry):
            first = steps - late + q * 2

            @pl.when(r == 0)
            def _():
                for n in range(2):
                    p_copy(first + n).wait_recv()

            partners = [[partner_of(1, first + n, i) for i in range(CHUNK)] for n in range(2)]
            work(*[[(partner, r) for partner in pair] for pair in partners])
            return carry

        lax.fori_loop(0, late // 2, turn, 0)
        for d in range(1, members):
            o_copy(d, r).start()
        return carry

    if late:
        lax.fori_loop(0, rows, row_body, 0)
    else:
        for r in range(rows):
            for d in range(1, members):
                o_copy(d, r).start()

    def project(a, carry):
        for r in range(rows):
            real_sum = jnp.zeros((tall, LANES), jnp.float32)
            imag_sum = jnp.zeros((tall, LANES), jnp.float32)
            for h in range(2):
                first, second = load(own_local * bands + a, 0, h), load(own_local * bands + a, 1, h)
                real_sum += first * total[r, 0, h] + second * total[r, 1, h]
                imag_sum += first * total[r, 1, h] - second * total[r, 0, h]
            lanes_of[r, 0, pl.ds(a, 1)] = jnp.sum(real_sum, axis=0, keepdims=True)
            lanes_of[r, 1, pl.ds(a, 1)] = jnp.sum(imag_sum, axis=0, keepdims=True)
        return carry

    lax.fori_loop(0, bands, project, 0)
    lane = lax.broadcasted_iota(jnp.int32, (bands, LANES), 1)
    level = lax.broadcasted_iota(jnp.int32, (bands, LANES), 0)
    entry = 2 * local * bands
    letter = jnp.zeros((bands, LANES), jnp.float32)
    for r in range(rows):
        at_band = lax.rem(first_row, bands) + r
        filled = jnp.where(at_band < counts[group * local + own_local], 1.0, 0.0).astype(jnp.float32)
        for part in range(2):
            value = jnp.sum(lanes_of[r, part], axis=1, keepdims=True) / volume
            letter = jnp.where(lane == (own_local * 2 + part) * bands + at_band, value, letter)
            if part == 0:
                term = jnp.where(level == at_band, value, 0.0) * (filled / (2.0 * groups * local))
                letter = letter + jnp.where(lane == entry, term, 0.0)
    mail[...] = letter
    mails[me] = letter

    def m_copy(d):
        to = lax.rem(me + d, members)
        return remote(mail, mails.at[me], m_send.at[d - 1], m_recv.at[d - 1], ga=to)

    for d in range(1, members):
        m_copy(d).start()

    own_part = pltpu.make_async_copy(total.at[:, :, :, pl.ds(pl.multiple_of(seat(me) * piece, piece), piece)],
                                     landing.at[pl.ds(lax.rem(me, share) * orbitals + first_row, rows)], local_sem.at[3])
    own_part.start()
    for d in range(1, members):
        m_copy(d).wait_recv()
    summed = jnp.sum(mails[...], axis=0)
    for l in range(local):
        for part in range(2):
            begin = (l * 2 + part) * bands
            matrix[l, part] = summed[:, begin:begin + bands]
    mine = jnp.where(lane == entry, summed, 0.0)
    note[...] = mine
    notes[group] = mine

    def e_copy(d):
        to = lax.rem(group + d, groups)
        return remote(note, notes.at[group], e_send.at[d - 1], e_recv.at[d - 1], ka=to)

    for d in range(1, groups):
        e_copy(d).start()

    own_part.wait()
    for r in range(rows):
        for d in range(1, members):
            o_copy(d, r).wait_recv()

    if share > 1:
        def add_up(o, carry):
            value = arrived[o]
            for n in range(1, share):
                value = value + arrived[n * orbitals + o]
            out[o] = value
            return carry

        lax.fori_loop(0, orbitals, add_up, 0)
    for d in range(1, groups):
        e_copy(d).wait_recv()
    energy[0, 0] = jnp.sum(notes[...])

    for d in offsets:
        @pl.when(inside(d))
        def _():
            wait_for(pieces.at[pl.ds(0, ready * CHUNK)] if far(d) else pieces, z_send.at[offsets.index(d)])
    if relayed:
        @pl.when((chip == 1) | (chip == chips - 2))
        def _():
            wait_for(pieces.at[pl.ds(0, (steps - ready) * CHUNK)], r_send.at[0])
    for d in range(1, chips):
        wait_for(pieces, x_send.at[d - 1])
        kz_copy(0, d).wait_send()
        kz_copy(1, d).wait_send()
    kd_copy(0).wait_send()
    kd_copy(1).wait_send()
    xo_copy.wait_send()

    def drain(j, carry):
        d_copy(j).wait_send()
        p_copy(j).wait_send()
        return carry

    lax.fori_loop(0, steps, drain, 0)
    for d in range(1, members):
        for r in range(rows):
            o_copy(d, r).wait_send()
        m_copy(d).wait_send()
    for d in range(1, groups):
        e_copy(d).wait_send()


def on_device(orbitals, band_counts, pair_slot, kernel):
    local, bands, _, planes, columns = orbitals.shape
    slots, points, width = kernel.shape
    members = lax.axis_size("ga")
    groups = lax.axis_size("ka")
    wide = LANES // points
    quads = points // (2 * wide)
    tall = quads * points
    tiles = columns // LANES
    count = local * bands
    rows = max(1, count // members)
    share = max(1, members // count)
    windows = 2 * local
    piece = tall // members
    steps = count // CHUNK
    chips = members // 2
    tables = build_tables(points, members)
    f32, bf16 = jnp.float32, jnp.bfloat16

    pieces = orbitals.reshape(count, 2, planes, tiles, LANES).transpose(0, 1, 3, 2, 4)
    pieces = pieces.reshape(count, 4, piece, LANES)

    smem = pl.BlockSpec(memory_space=pltpu.SMEM)
    vmem = pl.BlockSpec(memory_space=pltpu.VMEM)
    anywhere = pl.BlockSpec(memory_space=pl.ANY)
    dims = (local, bands, members, groups, points, planes)
    dma = pltpu.SemaphoreType.DMA
    out, matrix, energy = pl.pallas_call(
        functools.partial(exchange_kernel, dims),
        out_shape=(jax.ShapeDtypeStruct((count, 2, 2, piece, LANES), f32),
                   jax.ShapeDtypeStruct((local, 2, bands, bands), f32),
                   jax.ShapeDtypeStruct((1, 1), f32)),
        in_specs=[smem, smem, vmem, vmem] + [anywhere] * 5,
        out_specs=(vmem, vmem, smem),
        scratch_shapes=[
            pltpu.VMEM((2 * count, 2, chips, 4, piece, LANES), bf16),
            pltpu.VMEM(tables[0].shape, bf16), pltpu.VMEM(tables[1].shape, bf16),
            pltpu.VMEM(tables[2].shape, bf16), pltpu.VMEM(tables[3].shape, bf16),
            pltpu.VMEM(tables[4].shape, f32),
            pltpu.VMEM((local, windows, points, width), f32),
            pltpu.VMEM((2, 2, chips, local, points, width), f32),
            pltpu.VMEM((windows, 2 * tall, LANES), f32),
            pltpu.VMEM((rows, 2, 2, tall, LANES), f32),
            pltpu.VMEM((rows, 2, 2, tall, LANES), f32),
            pltpu.VMEM((share * count if share > 1 else 1, 2, 2, piece, LANES), f32),
            pltpu.VMEM((rows, 2, bands, LANES), f32),
            pltpu.VMEM((bands, LANES), f32),
            pltpu.VMEM((members, bands, LANES), f32),
            pltpu.VMEM((bands, LANES), f32),
            pltpu.VMEM((groups, bands, LANES), f32),
            dma((5,)), dma((4,)),
            dma((2 * chips - 2,)), dma((steps,)), dma((1,)), dma((steps,)), dma((steps,)), dma((1,)), dma((1,)),
            dma((chips - 1,)), dma((steps,)), dma((steps,)), dma((steps,)),
            dma((2, chips - 1)), dma((2,)), dma((2,)), dma((2,)),
            dma((rows, members - 1)), dma((rows, members - 1)), dma((members - 1,)), dma((members - 1,)),
            dma((groups - 1,)), dma((groups - 1,)),
        ],
        compiler_params=pltpu.CompilerParams(vmem_limit_bytes=56 * 2 ** 20, collective_id=0, has_side_effects=True),
        name="exchange",
    )(band_counts, pair_slot, pieces, kernel, *[jnp.asarray(table) for table in tables])
    out = out.reshape(local, bands, 2, tiles, planes, LANES).transpose(0, 1, 2, 4, 3, 5)
    return out.reshape(local, bands, 2, planes, columns), matrix, energy.reshape(())


def solution(mesh):
    in_specs = (P("ka", None, None, "ga", None), P(), P(), P(None, None, "ga"))
    out_specs = (P("ka", None, None, "ga", None), P("ka", None, None, None), P())
    return jax.shard_map(
        on_device, mesh=mesh, in_specs=in_specs, out_specs=out_specs, check_vma=False
    )
```

time: 108 us -> 72.5 us (0.67)
  the two profiles are of different devices: /device:TPU:16 before, /device:TPU:0 now
where the time goes in v2:
time: 72.5 us; the launch traced here: 72.4 us
  Pallas kernels  67.5 us (93%)
  local copies, waits for them, and re-layouts  2.5 us (3%)
  between operations  2.38 us (3%)
    pallas_call x1, Pallas kernels, on_device(): pl.pallas_call(functools.partial(exchange_kernel, dims), out_shape=(jax.S...  67.5 us
    unnamed x4, local copies, waits for them, and re-layouts  2.5 us

profile of v2, /device:TPU:0, one launch (start us, length us, event | category | flops | bytes accessed | tf_op | source)
XLA Modules:
  0.0 72.4 jit_solution(17115869030131630512)
XLA Ops:
  0.6 67.5 %exchange.1 = (f32[16,2,2,16,128]{4,3,2,1,0:T(8,128)}, f32[2,2,8,8]{3,2,1,0:T(8,128)}, f32[1,1]{1,0:T(1,128)}) custom-call(s32[8]{0:T(128)} %counts.1, s32[8,8]{1,0:T(8,128)} %slots.1, bf16[16,4,16,128]{3,2,1,0:T(8,128)(2,1)} %bitcast.12, f32[8,32,128]{2,1,0:T(8,128)} %kernel.1, bf16[4,128,384]{2,1,0:T(8,128)(2,1)} %constant.10.clone.left_in, ...), custom_call_target="tpu_custom_call" | custom-call | tf_op jit(solution)/shard_map/exchange/pallas_call | solution.py:619
  68.1 0.0 copy-start
  68.1 1.9 %copy.17 = f32[2,8,2,4,1024]{4,3,2,1,0:T(4,128)} copy(f32[2,8,2,4,1024]{4,3,2,1,0:T(4,128)} %bitcast.11) | data formatting | bytes 1048576
  70.0 0.0 copy-done
  70.0 0.6 copy.18
Async XLA Ops:
  68.1 1.9 %copy-start = (f32[2,2,8,8]{3,2,1,0:T(8,128)S(1)}, f32[2,2,8,8]{3,2,1,0:T(8,128)}, u32[]{:S(2)}) copy-start(f32[2,2,8,8]{3,2,1,0:T(8,128)} %get-tuple-element.13) | copy-start | bytes 3076

commit v3 on v2

--- a/solution.py
+++ b/solution.py
@@ -87,7 +87,6 @@
     piece = tall // members
     held = points // members
     volume = float(points ** 3)
-    scale = -1.0 / (groups * local * volume)
     ready = max(1, 2 * rows // CHUNK)
     lead = min(max(LEAD, ready), steps)
     late = SPLIT if rows > 1 else 0
@@ -123,22 +122,21 @@
         return pltpu.make_async_remote_copy(src_ref=src, dst_ref=dst, send_sem=send, recv_sem=recv,
                                             device_id=where, device_id_type=MESH)
 
-    table_copies = [pltpu.make_async_copy(src, dst, table_sem.at[i]) for i, (src, dst) in enumerate(
-        [(left_in, left), (left_back_in, left_back), (right_in, right), (right_back_in, right_back),
-         (twiddle_in, twiddle)])]
-    for copy in table_copies:
-        copy.start()
-    place = pltpu.make_async_copy(pieces, block.at[pl.ds(0, orbitals), core, chip], local_sem.at[0])
-    place.start()
-    for l in range(local):
-        for w in range(windows):
-            staged[l, w] = kernel[slots[group * local + l, window_kpoints[w]]] * scale
-
     barrier = pltpu.get_barrier_semaphore()
     for d in range(1, members):
         pl.semaphore_signal(barrier, inc=1, device_id={"ga": lax.rem(me + d, members)}, device_id_type=MESH)
     for d in range(1, groups):
         pl.semaphore_signal(barrier, inc=1, device_id={"ka": lax.rem(group + d, groups)}, device_id_type=MESH)
+
+    table_copies = [pltpu.make_async_copy(src, dst, table_sem.at[i]) for i, (src, dst) in enumerate(
+        [(left_in, left), (left_back_in, left_back), (right_in, right), (right_back_in, right_back),
+         (twiddle_in, twiddle)])]
+    place = pltpu.make_async_copy(pieces, block.at[pl.ds(0, orbitals), core, chip], local_sem.at[0])
+    place.start()
+    for l in range(local):
+        for w in range(windows):
+            staged[l, w] = kernel[slots[group * local + l, window_kpoints[w]]] * (1.0 / volume)
+
     pl.semaphore_wait(barrier, members + groups - 2)
 
     offsets = [d for d in range(1 - chips, chips) if d != 0]
@@ -176,16 +174,18 @@
         return remote(here, here, r_send.at[0], z_recv.at[j], ga=end * 2 + core)
 
     xo_copy = remote(pieces, block.at[pl.ds(orbitals, orbitals), core, chip], xo_send.at[0], xo_recv.at[0], ka=after)
+    for d in range(1, chips):
+        kz_copy(0, d).start()
     for j in range(ready):
         z_start(j, 0)
-    for d in range(1, chips):
-        kz_copy(0, d).start()
     xo_copy.start()
     for j in range(ready, lead):
         z_start(j, 0)
     for d in range(1, chips):
         kz_copy(1, d).start()
     lax.fori_loop(lead, steps, z_start, 0)
+    for copy in table_copies:
+        copy.start()
     kplaces = [pltpu.make_async_copy(staged.at[own_local, pl.ds(half * local, local)], raw.at[half, core, chip],
                                      local_sem.at[1 + half]) for half in range(2)]
     for copy in kplaces:
@@ -230,13 +230,9 @@
         wait_for(raw.at[half, 0, pl.ds(0, chips - 1)], kz_recv.at[half])
         kd_copy(half).start()
 
+    total[...] = jnp.zeros_like(total)
     place.wait()
-    for j in range(ready):
-        pass_own(j)
     pass_kernel(0)
-    for copy in table_copies:
-        copy.wait()
-    total[...] = jnp.zeros_like(total)
 
     each = points // members
 
@@ -254,7 +250,12 @@
                     multiplier[half * local + l, (c * deep + q) * points:(c * deep + q + 1) * points, :] = (
                         jnp.concatenate(parts, axis=1))
 
+    pass_own(0)
     lay_out(0)
+    for j in range(1, ready):
+        pass_own(j)
+    for copy in table_copies:
+        copy.wait()
 
     def load(slot, part, h):
         value = block[slot, :, :, part * 2 + h]
@@ -505,7 +506,7 @@
         at_band = lax.rem(first_row, bands) + r
         filled = jnp.where(at_band < counts[group * local + own_local], 1.0, 0.0).astype(jnp.float32)
         for part in range(2):
-            value = jnp.sum(lanes_of[r, part], axis=1, keepdims=True) / volume
+            value = jnp.sum(lanes_of[r, part], axis=1, keepdims=True) * (-1.0 / (groups * local * volume))
             letter = jnp.where(lane == (own_local * 2 + part) * bands + at_band, value, letter)
             if part == 0:
                 term = jnp.where(level == at_band, value, 0.0) * (filled / (2.0 * groups * local))
@@ -541,24 +542,6 @@
     for d in range(1, groups):
         e_copy(d).start()
 
-    own_part.wait()
-    for r in range(rows):
-        for d in range(1, members):
-            o_copy(d, r).wait_recv()
-
-    if share > 1:
-        def add_up(o, carry):
-            value = arrived[o]
-            for n in range(1, share):
-                value = value + arrived[n * orbitals + o]
-            out[o] = value
-            return carry
-
-        lax.fori_loop(0, orbitals, add_up, 0)
-    for d in range(1, groups):
-        e_copy(d).wait_recv()
-    energy[0, 0] = jnp.sum(notes[...])
-
     for d in offsets:
         @pl.when(inside(d))
         def _():
@@ -581,6 +564,24 @@
         return carry
 
     lax.fori_loop(0, steps, drain, 0)
+    own_part.wait()
+    for r in range(rows):
+        for d in range(1, members):
+            o_copy(d, r).wait_recv()
+
+    if share > 1:
+        def add_up(o, carry):
+            value = arrived[o]
+            for n in range(1, share):
+                value = value + arrived[n * orbitals + o]
+            out[o] = value
+            return carry
+
+        lax.fori_loop(0, orbitals, add_up, 0)
+    for d in range(1, groups):
+        e_copy(d).wait_recv()
+    energy[0, 0] = jnp.sum(notes[...])
+
     for d in range(1, members):
         for r in range(rows):
             o_copy(d, r).wait_send()
@@ -618,8 +619,8 @@
     dma = pltpu.SemaphoreType.DMA
     out, matrix, energy = pl.pallas_call(
         functools.partial(exchange_kernel, dims),
-        out_shape=(jax.ShapeDtypeStruct((count, 2, 2, piece, LANES), f32),
-                   jax.ShapeDtypeStruct((local, 2, bands, bands), f32),
+        out_shape=(pltpu.VMEM((count, 2, 2, piece, LANES), f32),
+                   pltpu.VMEM((local, 2, bands, bands), f32),
                    jax.ShapeDtypeStruct((1, 1), f32)),
         in_specs=[smem, smem, vmem, vmem] + [anywhere] * 5,
         out_specs=(vmem, vmem, smem),
@@ -650,7 +651,7 @@
         name="exchange",
     )(band_counts, pair_slot, pieces, kernel, *[jnp.asarray(table) for table in tables])
     out = out.reshape(local, bands, 2, tiles, planes, LANES).transpose(0, 1, 2, 4, 3, 5)
-    return out.reshape(local, bands, 2, planes, columns), matrix, energy.reshape(())
+    return out.reshape(local, bands, 2, planes, columns) * (-1.0 / (local * groups)), matrix, energy.reshape(())
 
 
 def solution(mesh):

time: 72.5 us -> 71.5 us (0.986)
  local copies, waits for them, and re-layouts: 2.5 us -> 0.6 us
  other arithmetic: 0 us -> 0.84 us
    unnamed x4 -> x1, local copies, waits for them, and re-layouts: 2.5 us -> 0.6 us
    mul x0 -> x1, other arithmetic: none -> 0.84 us  [on_device(): out.reshape(local, bands, 2, planes, columns) * (-1.0 / (local * groups))]
where the time goes in v3:
time: 71.5 us; the launch traced here: 71.4 us
  Pallas kernels  67.6 us (95%)
  between operations  2.33 us (3%)
  other arithmetic  0.84 us (1%)
    pallas_call x1, Pallas kernels, on_device(): pl.pallas_call(functools.partial(exchange_kernel, dims), out_shape=(pltpu...  67.6 us

profile of v3, /device:TPU:0, one launch (start us, length us, event | category | flops | bytes accessed | tf_op | source)
XLA Modules:
  0.0 71.4 jit_solution(17465280997395649064)
XLA Ops:
  0.6 67.6 %exchange.1 = (f32[16,2,2,16,128]{4,3,2,1,0:T(8,128)S(1)}, f32[2,2,8,8]{3,2,1,0:T(8,128)S(1)}, f32[1,1]{1,0:T(1,128)}) custom-call(s32[8]{0:T(128)} %counts.1, s32[8,8]{1,0:T(8,128)} %slots.1, bf16[16,4,16,128]{3,2,1,0:T(8,128)(2,1)} %bitcast.12, f32[8,32,128]{2,1,0:T(8,128)} %kernel.1, bf16[4,128,384]{2,1,0:T(8,128)(2,1)} %constant.12.clone.left_in, ...), custom_call_target="tpu_custom_call" | custom-call | tf_op jit(solution)/shard_map/exchange/pallas_call | solution.py:620
  68.2 0.8 %broadcast_multiply_fusion = f32[16,2,2,16,128]{4,3,2,1,0:T(8,128)} fusion(f32[16,2,2,16,128]{4,3,2,1,0:T(8,128)S(1)} %get-tuple-element.6), kind=kLoop, calls=%fused_computation | loop fusion | flops 131072 | bytes 1048576 | tf_op jit(solution)/shard_map/mul | solution.py:654
  69.1 0.6 copy.16

commit v4 on v3

--- a/solution.py
+++ b/solution.py
@@ -174,10 +174,10 @@
         return remote(here, here, r_send.at[0], z_recv.at[j], ga=end * 2 + core)
 
     xo_copy = remote(pieces, block.at[pl.ds(orbitals, orbitals), core, chip], xo_send.at[0], xo_recv.at[0], ka=after)
+    for j in range(ready):
+        z_start(j, 0)
     for d in range(1, chips):
         kz_copy(0, d).start()
-    for j in range(ready):
-        z_start(j, 0)
     xo_copy.start()
     for j in range(ready, lead):
         z_start(j, 0)
@@ -232,6 +232,8 @@
 
     total[...] = jnp.zeros_like(total)
     place.wait()
+    for j in range(ready):
+        pass_own(j)
     pass_kernel(0)
 
     each = points // members
@@ -250,10 +252,7 @@
                     multiplier[half * local + l, (c * deep + q) * points:(c * deep + q + 1) * points, :] = (
                         jnp.concatenate(parts, axis=1))
 
-    pass_own(0)
     lay_out(0)
-    for j in range(1, ready):
-        pass_own(j)
     for copy in table_copies:
         copy.wait()
 

time: 71.5 us -> 71 us (level)
  no operation moved by 1% of the time
where the time goes in v4:
time: 71 us; the launch traced here: 70.9 us
  Pallas kernels  67.1 us (95%)
  between operations  2.33 us (3%)
  other arithmetic  0.84 us (1%)
    pallas_call x1, Pallas kernels, on_device(): pl.pallas_call(functools.partial(exchange_kernel, dims), out_shape=(pltpu...  67.1 us

profile of v4, /device:TPU:0, one launch (start us, length us, event | category | flops | bytes accessed | tf_op | source)
XLA Modules:
  0.0 70.9 jit_solution(14257483731410247437)
XLA Ops:
  0.6 67.1 %exchange.1 = (f32[16,2,2,16,128]{4,3,2,1,0:T(8,128)S(1)}, f32[2,2,8,8]{3,2,1,0:T(8,128)S(1)}, f32[1,1]{1,0:T(1,128)}) custom-call(s32[8]{0:T(128)} %counts.1, s32[8,8]{1,0:T(8,128)} %slots.1, bf16[16,4,16,128]{3,2,1,0:T(8,128)(2,1)} %bitcast.12, f32[8,32,128]{2,1,0:T(8,128)} %kernel.1, bf16[4,128,384]{2,1,0:T(8,128)(2,1)} %constant.12.clone.left_in, ...), custom_call_target="tpu_custom_call" | custom-call | tf_op jit(solution)/shard_map/exchange/pallas_call | solution.py:619
  67.7 0.8 %broadcast_multiply_fusion = f32[16,2,2,16,128]{4,3,2,1,0:T(8,128)} fusion(f32[16,2,2,16,128]{4,3,2,1,0:T(8,128)S(1)} %get-tuple-element.6), kind=kLoop, calls=%fused_computation | loop fusion | flops 131072 | bytes 1048576 | tf_op jit(solution)/shard_map/mul | solution.py:653
  68.6 0.6 copy.16
